TPU v7x, 32 devices: a whole 2x2x4 slice. The times are simulated.
32 devices in a mesh: py: 4 (over y, x), px: 4 (over z), pz: 2 (over core).
Axes of the slice: x: 2, y: 2, z: 4, core: 2. Of those that a mesh axis runs over, the one named last changes fastest.
Arguments:
- tracer: float32 [32, 384, 16, 128], P('py', 'px', 'pz'), may hold values from 0.2 to 1.8
- flow_y: float32 [32, 384, 16, 128], P('py', 'px', 'pz'), may hold values from -0.3 to 0.3
- flow_x: float32 [32, 384, 16, 128], P('py', 'px', 'pz'), may hold values from -0.3 to 0.3
- flow_z: float32 [32, 384, 16, 128], P('py', 'px', 'pz'), may hold values from -0.3 to 0.3
Outputs:
- potential: float32 [32, 384, 16, 128], P('py', 'px', 'pz')
- tracer_end: float32 [32, 384, 16, 128], P('py', 'px', 'pz')
All inputs are finite; a program needn't handle non-finite values.
Results may differ from a plain program's by a relative error of at most 0.00002.
Values sent between devices are 32-bit elements; how exact they have to be, the bound alone decides.
A program may use at most 128 MiB of HBM per device.

v0:
```python
import jax
import jax.numpy as jnp
from jax import lax
from jax.sharding import PartitionSpec as P

STEPS = 4


def padded_2(block, sides, width):
    for axis, dim in sides:
        count = lax.axis_size(axis)
        forward = [(i, i + 1) for i in range(count - 1)]
        backward = [(target, source) for source, target in forward]
        low = lax.ppermute(
            lax.slice_in_dim(block, block.shape[dim] - width, None, axis=dim), axis, forward
        )
        high = lax.ppermute(lax.slice_in_dim(block, 0, width, axis=dim), axis, backward)
        block = jnp.concatenate([low, block, high], axis=dim)
    return block


def prefix(part, axis, combine, identity):
    place = lax.axis_index(axis)
    gathered = lax.all_gather(part, axis)
    state = jnp.zeros_like(part) + jnp.asarray(identity, part.dtype)

    def one(lap, state):
        return combine(state, lax.dynamic_index_in_dim(gathered, lap, 0, False))

    return lax.fori_loop(0, place, one, state)


def strip_edges(values, dims):
    for dim in dims:
        values = lax.slice_in_dim(values, 1, values.shape[dim] - 1, axis=dim)
    return values


def neighbour(values, dim, start, dims):
    others = [other for other in dims if other != dim]
    values = strip_edges(values, others)
    return lax.slice_in_dim(values, start, start + values.shape[dim] - 2, axis=dim)


def one_step(padded, flow_y, flow_x, flow_z):
    middle = strip_edges(padded, (0, 1, 2))
    lower = [neighbour(padded, dim, 0, (0, 1, 2)) for dim in (0, 1, 2)]
    upper = [neighbour(padded, dim, 2, (0, 1, 2)) for dim in (0, 1, 2)]
    slopes = [above - below for above, below in zip(upper, lower)]
    smooth_rate = 0.05
    spread = lower[0] + upper[0] + lower[1] + upper[1] + lower[2] + upper[2] - 6.0 * middle
    return (
        middle - flow_y * slopes[0] - flow_x * slopes[1] - flow_z * slopes[2] + smooth_rate * spread
    )


def local(tracer, flow_y, flow_x, flow_z):
    for step in range(STEPS):
        padded = padded_2(tracer, (("py", 0), ("px", 1), ("pz", 2)), 1)
        tracer = one_step(padded, flow_y, flow_x, flow_z)
    here = jnp.cumsum(tracer, axis=2)
    total = lax.slice_in_dim(here, here.shape[2] - 1, here.shape[2], axis=2)

    def add_pair(earlier_total, later_total):
        return earlier_total + later_total

    below = prefix(total, "pz", add_pair, jnp.zeros_like(total))
    potential = (here + below) / (tracer.shape[2] * lax.axis_size("pz"))
    return (potential, tracer)


def solution(mesh):
    placed = (
        P("py", "px", "pz", None),
        P("py", "px", "pz", None),
        P("py", "px", "pz", None),
        P("py", "px", "pz", None),
    )
    return jax.shard_map(
        local,
        mesh=mesh,
        in_specs=placed,
        out_specs=(P("py", "px", "pz", None), P("py", "px", "pz", None)),
        check_vma=False,
    )
```

profile of v0, /device:TPU:5, one launch (start us, length us, event | category | flops | bytes accessed | tf_op | source)
XLA Modules:
  0.0 193.0 jit_solution(10426126384780403158)
XLA Ops:
  9.5 6.6 %collective-permute-done.1 = f32[1,96,8,128]{3,1,2,0:T(8,128)S(1)} collective-permute-done((f32[1,96,8,128]{3,1,2,0:T(8,128)S(1)}, f32[1,96,8,128]{3,1,2,0:T(8,128)S(1)}, u32[]{:S(2)}, u32[]{:S(2)}) %collective-permute-start.1) | collective-permute-done | bytes 393248 | tf_op jit(solution)/shard_map/ppermute | solution.py:14
  16.8 5.9 %collective-permute-done = f32[1,96,8,128]{3,1,2,0:T(8,128)S(1)} collective-permute-done((f32[1,96,8,128]{3,1,2,0:T(8,128)S(1)}, f32[1,96,8,128]{3,1,2,0:T(8,128)S(1)}, u32[]{:S(2)}, u32[]{:S(2)}) %collective-permute-start) | collective-permute-done | bytes 393248 | tf_op jit(solution)/shard_map/ppermute | solution.py:17
  24.0 4.0 %collective-permute-start.3 = (f32[10,1,8,128]{3,1,2,0:T(1,128)S(1)}, f32[10,1,8,128]{3,1,2,0:T(1,128)S(1)}, u32[]{:S(2)}, u32[]{:S(2)}) collective-permute-start(f32[10,1,8,128]{3,1,2,0:T(1,128)S(1)} %get-tuple-element.58), channel_id=1, source_target_pairs={{0,2},{2,4},{4,6},{1,3},{3,5},{5,7},{8,10},{10,12},{12,14},{9,11},... | collective-permute-start | bytes 122888 | tf_op jit(solution)/shard_map/ppermute | solution.py:14
  29.2 4.6 %collective-permute-start.4 = (f32[10,98,1,128]{3,1,2,0:T(8,128)S(1)}, f32[10,98,1,128]{3,1,2,0:T(8,128)S(1)}, u32[]{:S(2)}, u32[]{:S(2)}) collective-permute-start(f32[10,98,1,128]{3,1,2,0:T(8,128)S(1)} %get-tuple-element.51), channel_id=1, source_target_pairs={{1,0},{3,2},{5,4},{7,6},{9,8},{11,10},{13,12},{15,14},{17,16},{19,... | collective-permute-start | bytes 1505288 | tf_op jit(solution)/shard_map/ppermute | solution.py:17
  37.7 9.8 %multiply_add_fusion.3 = f32[8,96,8,128]{3,1,2,0:T(8,128)S(1)} fusion(f32[8,96,8,128]{3,1,2,0:T(8,128)} %copy-done.3, f32[10,98,1,128]{3,1,2,0:T(8,128)S(1)} %collective-permute-done.4, f32[10,1,8,128]{3,1,2,0:T(1,128)S(1)} %collective-permute-done.2, f32[10,96,8,128]{3,1,2,0:T(8,128)S(1)} %constant_dynamic-update-slice_fusion, ...), kind=kLoop, calls=%fused_computation.69 | loop fusion | flops 22020096 | bytes 21532672 | tf_op jit(solution)/shard_map/add | solution.py:53
  47.5 5.0 %collective-permute-start.6 = (f32[1,96,8,128]{3,1,2,0:T(8,128)S(1)}, f32[1,96,8,128]{3,1,2,0:T(8,128)S(1)}, u32[]{:S(2)}, u32[]{:S(2)}) collective-permute-start(f32[1,96,8,128]{3,1,2,0:T(8,128)S(1)} %get-tuple-element.65), channel_id=1, source_target_pairs={{8,0},{16,8},{24,16},{9,1},{17,9},{25,17},{10,2},{18,10},{26,18},{... | collective-permute-start | bytes 1179656 | tf_op jit(solution)/shard_map/ppermute | solution.py:17
  54.5 6.4 %collective-permute-done.6 = f32[1,96,8,128]{3,1,2,0:T(8,128)S(1)} collective-permute-done((f32[1,96,8,128]{3,1,2,0:T(8,128)S(1)}, f32[1,96,8,128]{3,1,2,0:T(8,128)S(1)}, u32[]{:S(2)}, u32[]{:S(2)}) %collective-permute-start.6) | collective-permute-done | bytes 393248 | tf_op jit(solution)/shard_map/ppermute | solution.py:17
  60.9 9.4 %collective-permute-done.7 = f32[1,96,8,128]{3,1,2,0:T(8,128)S(1)} collective-permute-done((f32[1,96,8,128]{3,1,2,0:T(8,128)S(1)}, f32[1,96,8,128]{3,1,2,0:T(8,128)S(1)}, u32[]{:S(2)}, u32[]{:S(2)}) %collective-permute-start.7) | collective-permute-done | bytes 393248 | tf_op jit(solution)/shard_map/ppermute | solution.py:14
  71.7 4.6 %collective-permute-start.9 = (f32[10,1,8,128]{3,1,2,0:T(1,128)S(1)}, f32[10,1,8,128]{3,1,2,0:T(1,128)S(1)}, u32[]{:S(2)}, u32[]{:S(2)}) collective-permute-start(f32[10,1,8,128]{3,1,2,0:T(1,128)S(1)} %get-tuple-element.56), channel_id=1, source_target_pairs={{0,2},{2,4},{4,6},{1,3},{3,5},{5,7},{8,10},{10,12},{12,14},{9,11},... | collective-permute-start | bytes 122888 | tf_op jit(solution)/shard_map/ppermute | solution.py:14
  77.4 3.8 %collective-permute-start.10 = (f32[10,98,1,128]{3,1,2,0:T(8,128)S(1)}, f32[10,98,1,128]{3,1,2,0:T(8,128)S(1)}, u32[]{:S(2)}, u32[]{:S(2)}) collective-permute-start(f32[10,98,1,128]{3,1,2,0:T(8,128)S(1)} %get-tuple-element.49), channel_id=1, source_target_pairs={{1,0},{3,2},{5,4},{7,6},{9,8},{11,10},{13,12},{15,14},{17,16},{19,... | collective-permute-start | bytes 1505288 | tf_op jit(solution)/shard_map/ppermute | solution.py:17
  85.0 7.7 %multiply_add_fusion.2 = f32[8,96,8,128]{3,1,2,0:T(8,128)S(1)} fusion(f32[8,96,8,128]{3,1,2,0:T(8,128)S(1)} %multiply_add_fusion.3, f32[10,98,1,128]{3,1,2,0:T(8,128)S(1)} %collective-permute-done.10, f32[10,1,8,128]{3,1,2,0:T(1,128)S(1)} %collective-permute-done.8, f32[1,96,8,128]{3,1,2,0:T(8,128)S(1)} %collective-permute-done.6, ...), kind=kLoop, calls=%fused_computation.68 | loop fusion | flops 28311552 | bytes 17600512 | tf_op jit(solution)/shard_map/add | solution.py:53
  98.2 7.1 %collective-permute-done.12 = f32[1,96,8,128]{3,1,2,0:T(8,128)S(1)} collective-permute-done((f32[1,96,8,128]{3,1,2,0:T(8,128)S(1)}, f32[1,96,8,128]{3,1,2,0:T(8,128)S(1)}, u32[]{:S(2)}, u32[]{:S(2)}) %collective-permute-start.12) | collective-permute-done | bytes 393248 | tf_op jit(solution)/shard_map/ppermute | solution.py:17
  105.3 6.5 %collective-permute-done.13 = f32[1,96,8,128]{3,1,2,0:T(8,128)S(1)} collective-permute-done((f32[1,96,8,128]{3,1,2,0:T(8,128)S(1)}, f32[1,96,8,128]{3,1,2,0:T(8,128)S(1)}, u32[]{:S(2)}, u32[]{:S(2)}) %collective-permute-start.13) | collective-permute-done | bytes 393248 | tf_op jit(solution)/shard_map/ppermute | solution.py:14
  113.1 4.6 %collective-permute-start.15 = (f32[10,1,8,128]{3,1,2,0:T(1,128)S(1)}, f32[10,1,8,128]{3,1,2,0:T(1,128)S(1)}, u32[]{:S(2)}, u32[]{:S(2)}) collective-permute-start(f32[10,1,8,128]{3,1,2,0:T(1,128)S(1)} %get-tuple-element.54), channel_id=1, source_target_pairs={{0,2},{2,4},{4,6},{1,3},{3,5},{5,7},{8,10},{10,12},{12,14},{9,11},... | collective-permute-start | bytes 122888 | tf_op jit(solution)/shard_map/ppermute | solution.py:14
  118.9 3.5 %collective-permute-start.16 = (f32[10,98,1,128]{3,1,2,0:T(8,128)S(1)}, f32[10,98,1,128]{3,1,2,0:T(8,128)S(1)}, u32[]{:S(2)}, u32[]{:S(2)}) collective-permute-start(f32[10,98,1,128]{3,1,2,0:T(8,128)S(1)} %get-tuple-element.47), channel_id=1, source_target_pairs={{1,0},{3,2},{5,4},{7,6},{9,8},{11,10},{13,12},{15,14},{17,16},{19,... | collective-permute-start | bytes 1505288 | tf_op jit(solution)/shard_map/ppermute | solution.py:17
  126.2 7.8 %multiply_add_fusion.1 = f32[8,96,8,128]{3,1,2,0:T(8,128)S(1)} fusion(f32[8,96,8,128]{3,1,2,0:T(8,128)S(1)} %multiply_add_fusion.2, f32[10,98,1,128]{3,1,2,0:T(8,128)S(1)} %collective-permute-done.16, f32[10,1,8,128]{3,1,2,0:T(1,128)S(1)} %collective-permute-done.14, f32[1,96,8,128]{3,1,2,0:T(8,128)S(1)} %collective-permute-done.12, ...), kind=kLoop, calls=%fused_computation.67 | loop fusion | flops 28311552 | bytes 17600512 | tf_op jit(solution)/shard_map/add | solution.py:53
  136.0 3.5 %collective-permute-start.19 = (f32[1,96,8,128]{3,1,2,0:T(8,128)S(1)}, f32[1,96,8,128]{3,1,2,0:T(8,128)S(1)}, u32[]{:S(2)}, u32[]{:S(2)}) collective-permute-start(f32[1,96,8,128]{3,1,2,0:T(8,128)S(1)} %get-tuple-element.60), channel_id=1, source_target_pairs={{0,8},{8,16},{16,24},{1,9},{9,17},{17,25},{2,10},{10,18},{18,26},{... | collective-permute-start | bytes 1179656 | tf_op jit(solution)/shard_map/ppermute | solution.py:14
  139.6 7.2 %collective-permute-done.18 = f32[1,96,8,128]{3,1,2,0:T(8,128)S(1)} collective-permute-done((f32[1,96,8,128]{3,1,2,0:T(8,128)S(1)}, f32[1,96,8,128]{3,1,2,0:T(8,128)S(1)}, u32[]{:S(2)}, u32[]{:S(2)}) %collective-permute-start.18) | collective-permute-done | bytes 393248 | tf_op jit(solution)/shard_map/ppermute | solution.py:17
  146.8 6.3 %collective-permute-done.19 = f32[1,96,8,128]{3,1,2,0:T(8,128)S(1)} collective-permute-done((f32[1,96,8,128]{3,1,2,0:T(8,128)S(1)}, f32[1,96,8,128]{3,1,2,0:T(8,128)S(1)}, u32[]{:S(2)}, u32[]{:S(2)}) %collective-permute-start.19) | collective-permute-done | bytes 393248 | tf_op jit(solution)/shard_map/ppermute | solution.py:14
  154.4 4.6 %collective-permute-start.21 = (f32[10,1,8,128]{3,1,2,0:T(1,128)S(1)}, f32[10,1,8,128]{3,1,2,0:T(1,128)S(1)}, u32[]{:S(2)}, u32[]{:S(2)}) collective-permute-start(f32[10,1,8,128]{3,1,2,0:T(1,128)S(1)} %get-tuple-element.52), channel_id=1, source_target_pairs={{0,2},{2,4},{4,6},{1,3},{3,5},{5,7},{8,10},{10,12},{12,14},{9,11},... | collective-permute-start | bytes 122888 | tf_op jit(solution)/shard_map/ppermute | solution.py:14
  161.2 4.3 %collective-permute-start.22 = (f32[10,98,1,128]{3,1,2,0:T(8,128)}, f32[10,98,1,128]{3,1,2,0:T(8,128)}, u32[]{:S(2)}, u32[]{:S(2)}) collective-permute-start(f32[10,98,1,128]{3,1,2,0:T(8,128)} %get-tuple-element.45), channel_id=1, source_target_pairs={{1,0},{3,2},{5,4},{7,6},{9,8},{11,10},{13,12},{15,14},{17,16},{19,... | collective-permute-start | bytes 1505288 | tf_op jit(solution)/shard_map/ppermute | solution.py:17
  169.6 8.5 %multiply_add_fusion = f32[8,96,8,128]{3,1,2,0:T(8,128)S(1)} fusion(f32[8,96,8,128]{3,1,2,0:T(8,128)S(1)} %multiply_add_fusion.1, f32[10,98,1,128]{3,1,2,0:T(8,128)} %collective-permute-done.22, f32[10,1,8,128]{3,1,2,0:T(1,128)} %copy-done.6, f32[1,96,8,128]{3,1,2,0:T(8,128)S(1)} %collective-permute-done.18, f32[1,96,8,128]{3,1,2,0:T(8,128)} %copy-done.5, ...), kind=kLoop, calls=%fused_computation.66 | loop fusion | flops 28311552 | bytes 17600512 | tf_op jit(solution)/shard_map/add | solution.py:53
  181.4 3.4 %copy.28 = f32[8,96,8,128]{3,2,1,0:T(8,128)} copy(f32[8,96,8,128]{3,1,2,0:T(8,128)S(1)} %multiply_add_fusion) | data formatting | bytes 6291456
  189.5 3.4 %copy.27 = f32[8,96,8,128]{3,2,1,0:T(8,128)} copy(f32[8,96,8,128]{3,1,2,0:T(8,128)S(1)} %add_multiply_fusion) | data formatting | bytes 6291456
  (70 shorter events, 54.8 us)
Async XLA Ops:
  3.3 12.8 %collective-permute-start.1 = (f32[1,96,8,128]{3,1,2,0:T(8,128)S(1)}, f32[1,96,8,128]{3,1,2,0:T(8,128)S(1)}, u32[]{:S(2)}, u32[]{:S(2)}) collective-permute-start(f32[1,96,8,128]{3,1,2,0:T(8,128)S(1)} %get-tuple-element.67), channel_id=1, source_target_pairs={{0,8},{8,16},{16,24},{1,9},{9,17},{17,25},{2,10},{10,18},{18,26},{... | collective-permute-start | bytes 1179656 | tf_op jit(solution)/shard_map/ppermute | solution.py:14
  6.4 16.2 %collective-permute-start = (f32[1,96,8,128]{3,1,2,0:T(8,128)S(1)}, f32[1,96,8,128]{3,1,2,0:T(8,128)S(1)}, u32[]{:S(2)}, u32[]{:S(2)}) collective-permute-start(f32[1,96,8,128]{3,1,2,0:T(8,128)S(1)} %get-tuple-element.66), channel_id=1, source_target_pairs={{8,0},{16,8},{24,16},{9,1},{17,9},{25,17},{10,2},{18,10},{26,18},{... | collective-permute-start | bytes 1179656 | tf_op jit(solution)/shard_map/ppermute | solution.py:17
  22.7 5.3 %collective-permute-start.2 = (f32[10,1,8,128]{3,1,2,0:T(1,128)S(1)}, f32[10,1,8,128]{3,1,2,0:T(1,128)S(1)}, u32[]{:S(2)}, u32[]{:S(2)}) collective-permute-start(f32[10,1,8,128]{3,1,2,0:T(1,128)S(1)} %get-tuple-element.59), channel_id=1, source_target_pairs={{2,0},{4,2},{6,4},{3,1},{5,3},{7,5},{10,8},{12,10},{14,12},{11,9},... | collective-permute-start | bytes 122888 | tf_op jit(solution)/shard_map/ppermute | solution.py:17
  24.0 5.1 %collective-permute-start.3 = (f32[10,1,8,128]{3,1,2,0:T(1,128)S(1)}, f32[10,1,8,128]{3,1,2,0:T(1,128)S(1)}, u32[]{:S(2)}, u32[]{:S(2)}) collective-permute-start(f32[10,1,8,128]{3,1,2,0:T(1,128)S(1)} %get-tuple-element.58), channel_id=1, source_target_pairs={{0,2},{2,4},{4,6},{1,3},{3,5},{5,7},{8,10},{10,12},{12,14},{9,11},... | collective-permute-start | bytes 122888 | tf_op jit(solution)/shard_map/ppermute | solution.py:14
  29.2 6.1 %collective-permute-start.4 = (f32[10,98,1,128]{3,1,2,0:T(8,128)S(1)}, f32[10,98,1,128]{3,1,2,0:T(8,128)S(1)}, u32[]{:S(2)}, u32[]{:S(2)}) collective-permute-start(f32[10,98,1,128]{3,1,2,0:T(8,128)S(1)} %get-tuple-element.51), channel_id=1, source_target_pairs={{1,0},{3,2},{5,4},{7,6},{9,8},{11,10},{13,12},{15,14},{17,16},{19,... | collective-permute-start | bytes 1505288 | tf_op jit(solution)/shard_map/ppermute | solution.py:17
  33.8 3.8 %collective-permute-start.5 = (f32[10,98,1,128]{3,1,2,0:T(8,128)S(1)}, f32[10,98,1,128]{3,1,2,0:T(8,128)S(1)}, u32[]{:S(2)}, u32[]{:S(2)}) collective-permute-start(f32[10,98,1,128]{3,1,2,0:T(8,128)S(1)} %get-tuple-element.50), channel_id=1, source_target_pairs={{0,1},{2,3},{4,5},{6,7},{8,9},{10,11},{12,13},{14,15},{16,17},{18,... | collective-permute-start | bytes 1505288 | tf_op jit(solution)/shard_map/ppermute | solution.py:14
  47.5 13.3 %collective-permute-start.6 = (f32[1,96,8,128]{3,1,2,0:T(8,128)S(1)}, f32[1,96,8,128]{3,1,2,0:T(8,128)S(1)}, u32[]{:S(2)}, u32[]{:S(2)}) collective-permute-start(f32[1,96,8,128]{3,1,2,0:T(8,128)S(1)} %get-tuple-element.65), channel_id=1, source_target_pairs={{8,0},{16,8},{24,16},{9,1},{17,9},{25,17},{10,2},{18,10},{26,18},{... | collective-permute-start | bytes 1179656 | tf_op jit(solution)/shard_map/ppermute | solution.py:17
  52.5 17.7 %collective-permute-start.7 = (f32[1,96,8,128]{3,1,2,0:T(8,128)S(1)}, f32[1,96,8,128]{3,1,2,0:T(8,128)S(1)}, u32[]{:S(2)}, u32[]{:S(2)}) collective-permute-start(f32[1,96,8,128]{3,1,2,0:T(8,128)S(1)} %get-tuple-element.64), channel_id=1, source_target_pairs={{0,8},{8,16},{16,24},{1,9},{9,17},{17,25},{2,10},{10,18},{18,26},{... | collective-permute-start | bytes 1179656 | tf_op jit(solution)/shard_map/ppermute | solution.py:14
  70.4 5.9 %collective-permute-start.8 = (f32[10,1,8,128]{3,1,2,0:T(1,128)S(1)}, f32[10,1,8,128]{3,1,2,0:T(1,128)S(1)}, u32[]{:S(2)}, u32[]{:S(2)}) collective-permute-start(f32[10,1,8,128]{3,1,2,0:T(1,128)S(1)} %get-tuple-element.57), channel_id=1, source_target_pairs={{2,0},{4,2},{6,4},{3,1},{5,3},{7,5},{10,8},{12,10},{14,12},{11,9},... | collective-permute-start | bytes 122888 | tf_op jit(solution)/shard_map/ppermute | solution.py:17
  71.7 5.7 %collective-permute-start.9 = (f32[10,1,8,128]{3,1,2,0:T(1,128)S(1)}, f32[10,1,8,128]{3,1,2,0:T(1,128)S(1)}, u32[]{:S(2)}, u32[]{:S(2)}) collective-permute-start(f32[10,1,8,128]{3,1,2,0:T(1,128)S(1)} %get-tuple-element.56), channel_id=1, source_target_pairs={{0,2},{2,4},{4,6},{1,3},{3,5},{5,7},{8,10},{10,12},{12,14},{9,11},... | collective-permute-start | bytes 122888 | tf_op jit(solution)/shard_map/ppermute | solution.py:14
  77.4 5.3 %collective-permute-start.10 = (f32[10,98,1,128]{3,1,2,0:T(8,128)S(1)}, f32[10,98,1,128]{3,1,2,0:T(8,128)S(1)}, u32[]{:S(2)}, u32[]{:S(2)}) collective-permute-start(f32[10,98,1,128]{3,1,2,0:T(8,128)S(1)} %get-tuple-element.49), channel_id=1, source_target_pairs={{1,0},{3,2},{5,4},{7,6},{9,8},{11,10},{13,12},{15,14},{17,16},{19,... | collective-permute-start | bytes 1505288 | tf_op jit(solution)/shard_map/ppermute | solution.py:17
  81.2 3.8 %collective-permute-start.11 = (f32[10,98,1,128]{3,1,2,0:T(8,128)S(1)}, f32[10,98,1,128]{3,1,2,0:T(8,128)S(1)}, u32[]{:S(2)}, u32[]{:S(2)}) collective-permute-start(f32[10,98,1,128]{3,1,2,0:T(8,128)S(1)} %get-tuple-element.48), channel_id=1, source_target_pairs={{0,1},{2,3},{4,5},{6,7},{8,9},{10,11},{12,13},{14,15},{16,17},{18,... | collective-permute-start | bytes 1505288 | tf_op jit(solution)/shard_map/ppermute | solution.py:14
  92.8 12.4 %collective-permute-start.12 = (f32[1,96,8,128]{3,1,2,0:T(8,128)S(1)}, f32[1,96,8,128]{3,1,2,0:T(8,128)S(1)}, u32[]{:S(2)}, u32[]{:S(2)}) collective-permute-start(f32[1,96,8,128]{3,1,2,0:T(8,128)S(1)} %get-tuple-element.63), channel_id=1, source_target_pairs={{8,0},{16,8},{24,16},{9,1},{17,9},{25,17},{10,2},{18,10},{26,18},{... | collective-permute-start | bytes 1179656 | tf_op jit(solution)/shard_map/ppermute | solution.py:17
  94.8 17.0 %collective-permute-start.13 = (f32[1,96,8,128]{3,1,2,0:T(8,128)S(1)}, f32[1,96,8,128]{3,1,2,0:T(8,128)S(1)}, u32[]{:S(2)}, u32[]{:S(2)}) collective-permute-start(f32[1,96,8,128]{3,1,2,0:T(8,128)S(1)} %get-tuple-element.62), channel_id=1, source_target_pairs={{0,8},{8,16},{16,24},{1,9},{9,17},{17,25},{2,10},{10,18},{18,26},{... | collective-permute-start | bytes 1179656 | tf_op jit(solution)/shard_map/ppermute | solution.py:14
  111.8 5.9 %collective-permute-start.14 = (f32[10,1,8,128]{3,1,2,0:T(1,128)S(1)}, f32[10,1,8,128]{3,1,2,0:T(1,128)S(1)}, u32[]{:S(2)}, u32[]{:S(2)}) collective-permute-start(f32[10,1,8,128]{3,1,2,0:T(1,128)S(1)} %get-tuple-element.55), channel_id=1, source_target_pairs={{2,0},{4,2},{6,4},{3,1},{5,3},{7,5},{10,8},{12,10},{14,12},{11,9},... | collective-permute-start | bytes 122888 | tf_op jit(solution)/shard_map/ppermute | solution.py:17
  113.1 5.7 %collective-permute-start.15 = (f32[10,1,8,128]{3,1,2,0:T(1,128)S(1)}, f32[10,1,8,128]{3,1,2,0:T(1,128)S(1)}, u32[]{:S(2)}, u32[]{:S(2)}) collective-permute-start(f32[10,1,8,128]{3,1,2,0:T(1,128)S(1)} %get-tuple-element.54), channel_id=1, source_target_pairs={{0,2},{2,4},{4,6},{1,3},{3,5},{5,7},{8,10},{10,12},{12,14},{9,11},... | collective-permute-start | bytes 122888 | tf_op jit(solution)/shard_map/ppermute | solution.py:14
  118.9 5.0 %collective-permute-start.16 = (f32[10,98,1,128]{3,1,2,0:T(8,128)S(1)}, f32[10,98,1,128]{3,1,2,0:T(8,128)S(1)}, u32[]{:S(2)}, u32[]{:S(2)}) collective-permute-start(f32[10,98,1,128]{3,1,2,0:T(8,128)S(1)} %get-tuple-element.47), channel_id=1, source_target_pairs={{1,0},{3,2},{5,4},{7,6},{9,8},{11,10},{13,12},{15,14},{17,16},{19,... | collective-permute-start | bytes 1505288 | tf_op jit(solution)/shard_map/ppermute | solution.py:17
  122.4 3.8 %collective-permute-start.17 = (f32[10,98,1,128]{3,1,2,0:T(8,128)S(1)}, f32[10,98,1,128]{3,1,2,0:T(8,128)S(1)}, u32[]{:S(2)}, u32[]{:S(2)}) collective-permute-start(f32[10,98,1,128]{3,1,2,0:T(8,128)S(1)} %get-tuple-element.46), channel_id=1, source_target_pairs={{0,1},{2,3},{4,5},{6,7},{8,9},{10,11},{12,13},{14,15},{16,17},{18,... | collective-permute-start | bytes 1505288 | tf_op jit(solution)/shard_map/ppermute | solution.py:14
  134.1 12.7 %collective-permute-start.18 = (f32[1,96,8,128]{3,1,2,0:T(8,128)S(1)}, f32[1,96,8,128]{3,1,2,0:T(8,128)S(1)}, u32[]{:S(2)}, u32[]{:S(2)}) collective-permute-start(f32[1,96,8,128]{3,1,2,0:T(8,128)S(1)} %get-tuple-element.61), channel_id=1, source_target_pairs={{8,0},{16,8},{24,16},{9,1},{17,9},{25,17},{10,2},{18,10},{26,18},{... | collective-permute-start | bytes 1179656 | tf_op jit(solution)/shard_map/ppermute | solution.py:17
  136.0 17.0 %collective-permute-start.19 = (f32[1,96,8,128]{3,1,2,0:T(8,128)S(1)}, f32[1,96,8,128]{3,1,2,0:T(8,128)S(1)}, u32[]{:S(2)}, u32[]{:S(2)}) collective-permute-start(f32[1,96,8,128]{3,1,2,0:T(8,128)S(1)} %get-tuple-element.60), channel_id=1, source_target_pairs={{0,8},{8,16},{16,24},{1,9},{9,17},{17,25},{2,10},{10,18},{18,26},{... | collective-permute-start | bytes 1179656 | tf_op jit(solution)/shard_map/ppermute | solution.py:14
  153.1 5.9 %collective-permute-start.20 = (f32[10,1,8,128]{3,1,2,0:T(1,128)S(1)}, f32[10,1,8,128]{3,1,2,0:T(1,128)S(1)}, u32[]{:S(2)}, u32[]{:S(2)}) collective-permute-start(f32[10,1,8,128]{3,1,2,0:T(1,128)S(1)} %get-tuple-element.53), channel_id=1, source_target_pairs={{2,0},{4,2},{6,4},{3,1},{5,3},{7,5},{10,8},{12,10},{14,12},{11,9},... | collective-permute-start | bytes 122888 | tf_op jit(solution)/shard_map/ppermute | solution.py:17
  154.4 5.7 %collective-permute-start.21 = (f32[10,1,8,128]{3,1,2,0:T(1,128)S(1)}, f32[10,1,8,128]{3,1,2,0:T(1,128)S(1)}, u32[]{:S(2)}, u32[]{:S(2)}) collective-permute-start(f32[10,1,8,128]{3,1,2,0:T(1,128)S(1)} %get-tuple-element.52), channel_id=1, source_target_pairs={{0,2},{2,4},{4,6},{1,3},{3,5},{5,7},{8,10},{10,12},{12,14},{9,11},... | collective-permute-start | bytes 122888 | tf_op jit(solution)/shard_map/ppermute | solution.py:14
  161.2 5.7 %collective-permute-start.22 = (f32[10,98,1,128]{3,1,2,0:T(8,128)}, f32[10,98,1,128]{3,1,2,0:T(8,128)}, u32[]{:S(2)}, u32[]{:S(2)}) collective-permute-start(f32[10,98,1,128]{3,1,2,0:T(8,128)} %get-tuple-element.45), channel_id=1, source_target_pairs={{1,0},{3,2},{5,4},{7,6},{9,8},{11,10},{13,12},{15,14},{17,16},{19,... | collective-permute-start | bytes 1505288 | tf_op jit(solution)/shard_map/ppermute | solution.py:17
  165.4 4.1 %collective-permute-start.23 = (f32[10,98,1,128]{3,1,2,0:T(8,128)}, f32[10,98,1,128]{3,1,2,0:T(8,128)}, u32[]{:S(2)}, u32[]{:S(2)}) collective-permute-start(f32[10,98,1,128]{3,1,2,0:T(8,128)} %get-tuple-element.44), channel_id=1, source_target_pairs={{0,1},{2,3},{4,5},{6,7},{8,9},{10,11},{12,13},{14,15},{16,17},{18,... | collective-permute-start | bytes 1505288 | tf_op jit(solution)/shard_map/ppermute | solution.py:14
  (8 other events, 108.5 us)
where the time goes:
time: 196 us; the launch traced here: 193 us
  waiting for transfers between devices  69.9 us (36%)
  starting transfers between devices  68.2 us (35%)
  other arithmetic  39.5 us (20%)
  local copies, waits for them, and re-layouts  11.7 us (6%)
  blocking collectives  2.5 us (1%)
    ppermute x12, waiting for transfers between devices, padded_2(): lax.ppermute(lax.slice_in_dim(block, block.shape[dim] - width, None, axis...  42.7 us
    ppermute x12, starting transfers between devices, padded_2(): lax.ppermute(lax.slice_in_dim(block, block.shape[dim] - width, None, axis...  35 us
    add x4, other arithmetic, one_step(): middle - flow_y * slopes[0] - flow_x * slopes[1] - flow_z * slopes[2]  33.9 us
    ppermute x12, starting transfers between devices, padded_2(): lax.ppermute(lax.slice_in_dim(block, 0, width, axis=dim), axis, backward)  33.2 us
    ppermute x12, waiting for transfers between devices, padded_2(): lax.ppermute(lax.slice_in_dim(block, 0, width, axis=dim), axis, backward)  27.2 us
    unnamed x21, local copies, waits for them, and re-layouts  10.1 us
  transfers between devices with their start and end apart: 24, of which 19 were waited for; matrix products, arithmetic and copies ran while one was open for 0% of the time, Pallas kernels for 0%

commit v1 on v0

v1 whole, which is shorter than its diff:
```python
import functools

import jax
import jax.numpy as jnp
from jax import lax
from jax.experimental import pallas as pl
from jax.experimental.pallas import tpu as pltpu
from jax.sharding import PartitionSpec as P

STEPS = 4
MESH = pl.DeviceIdType.MESH


def divisor(size, most):
    return max(d for d in range(1, most + 1) if size % d == 0)


class Axis:
    def __init__(self, name, count):
        self.name = name
        self.me = lax.axis_index(name)
        self.to = (self.me - 1, self.me + 1)
        self.sends = (self.me > 0, self.me < count - 1)
        self.gets = (self.sends[1], self.sends[0])


def kernel(counts, chunk, sub, tr, fy, fx, fz, pot, end, T, E, S, F, Z, load, ys, yr, xs, xr, zs, zr, zbs, zbr, eo, po, ebo, pbo):
    rows, width, depth, lanes = tr.shape
    chunks = width // chunk
    ay, ax, az = (Axis(n, c) for n, c in zip(("py", "px", "pz"), counts))
    flows = (fy, fx, fz)
    inner = rows - 2

    loads = [pltpu.make_async_copy(tr, T.at[0, pl.ds(1, rows), pl.ds(1, width)], load.at[0])]
    loads += [pltpu.make_async_copy(f, F.at[i], load.at[1 + i]) for i, f in enumerate(flows)]
    for copy in loads:
        copy.start()

    barrier = pltpu.get_barrier_semaphore()
    expect = 0
    for axis in (ay, ax, az):
        for d in (0, 1):
            @pl.when(axis.sends[d])
            def _():
                pl.semaphore_signal(barrier, inc=1, device_id={axis.name: axis.to[d]}, device_id_type=MESH)
            expect = expect + axis.sends[d].astype(jnp.int32)

    def blank(t):
        for d in (0, 1):
            @pl.when(jnp.logical_not(ay.gets[d]))
            def _():
                @pl.loop(0, chunks)
                def _(c):
                    T[t, rows + 1 if d == 0 else 0, pl.ds(1 + c * chunk, chunk)] = jnp.zeros((chunk, depth, lanes), jnp.float32)

            @pl.when(jnp.logical_not(ax.gets[d]))
            def _():
                T[t, pl.ds(1, rows), pl.ds(width + 1 if d == 0 else 0, 1)] = jnp.zeros((rows, 1, depth, lanes), jnp.float32)

    for t in range(STEPS):
        blank(t)
    pl.semaphore_wait(barrier, expect)

    def remote(src, dst, ssem, rsem, axis, d):
        return pltpu.make_async_remote_copy(
            src_ref=src, dst_ref=dst, send_sem=ssem, recv_sem=rsem,
            device_id={axis.name: axis.to[d]}, device_id_type=MESH,
        )

    def ycopy(t, d, c):
        at = c * chunk
        if t == 0:
            src = tr.at[0 if d == 0 else rows - 1, pl.ds(at, chunk)]
        else:
            src = T.at[t, 1 if d == 0 else rows, pl.ds(1 + at, chunk)]
        dst = T.at[t, rows + 1 if d == 0 else 0, pl.ds(1 + at, chunk)]
        return remote(src, dst, ys.at[t, d, c], yr.at[t, d, c], ay, d)

    def xcopy(t, d):
        if t == 0:
            src = tr.at[:, pl.ds(0 if d == 0 else width - 1, 1)]
        else:
            src = T.at[t, pl.ds(1, rows), pl.ds(1 if d == 0 else width, 1)]
        dst = T.at[t, pl.ds(1, rows), pl.ds(width + 1 if d == 0 else 0, 1)]
        return remote(src, dst, xs.at[t, d], xr.at[t, d], ax, d)

    def zrefs(t, d, y, ny, x, nx):
        row = pl.ds(0 if d == 0 else depth - 1, 1)
        if t < STEPS:
            src = T.at[t, pl.ds(1 + y, ny), pl.ds(1 + x, nx), row]
        else:
            src = S.at[pl.ds(y, ny), pl.ds(x, nx), row]
        return src, Z.at[t, pl.ds(y, ny), pl.ds(x, nx), row]

    def zcopy(t, d):
        return remote(*zrefs(t, d, 1, inner, 0, width), zs.at[t, d], zr.at[t, d], az, d)

    def zbcopy(t, d, c, b):
        return remote(
            *zrefs(t, d, 0 if b == 0 else rows - 1, 1, c * chunk, chunk),
            zbs.at[t, d, c, b], zbr.at[t, d, c, b], az, d,
        )

    def start(flag, copy):
        @pl.when(flag)
        def _():
            copy.start()

    def arrived(flag, copy):
        @pl.when(flag)
        def _():
            copy.wait_recv()

    level = lax.broadcasted_iota(jnp.int32, (sub, depth, lanes), 1)
    known = (level == jnp.where(az.gets[0], 0, -1)) | (level == jnp.where(az.gets[1], depth - 1, -1))
    first, last = level == 0, level == depth - 1
    share = 1.0 / (depth * counts[2])

    def cells(t, y, x):
        line = T[t, 1 + y, pl.ds(x, sub + 2)]
        here, x_low, x_high = line[1:-1], line[:-2], line[2:]
        y_low = T[t, y, pl.ds(1 + x, sub)]
        y_high = T[t, y + 2, pl.ds(1 + x, sub)]
        beside = jnp.where(known, Z[t, y, pl.ds(x, sub)], 0.0)
        z_low = pltpu.roll(jnp.where(last, beside, here), 1, 1)
        z_high = pltpu.roll(jnp.where(first, beside, here), depth - 1, 1)
        spread = y_low + y_high + x_low + x_high + z_low + z_high - 6.0 * here
        new = (
            here - F[0, y, pl.ds(x, sub)] * (y_high - y_low) - F[1, y, pl.ds(x, sub)] * (x_high - x_low)
            - F[2, y, pl.ds(x, sub)] * (z_high - z_low) + 0.05 * spread
        )
        if t < STEPS - 1:
            T[t + 1, 1 + y, pl.ds(1 + x, sub)] = new
        else:
            E[y, pl.ds(x, sub)] = new
            total, reach = new, 1
            while reach < depth:
                total = total + jnp.where(level >= reach, pltpu.roll(total, reach, 1), 0.0)
                reach *= 2
            S[y, pl.ds(x, sub)] = total * share

    def add_below(y, x):
        low = Z[STEPS, y, pl.ds(x, sub), pl.ds(depth - 1, 1)]
        S[y, pl.ds(x, sub)] = S[y, pl.ds(x, sub)] + low

    def out(ref, to, y, ny, x, nx, sem):
        return pltpu.make_async_copy(
            ref.at[pl.ds(y, ny), pl.ds(x, nx)], to.at[pl.ds(y, ny), pl.ds(x, nx)], sem
        )

    def ends(c, b):
        return out(E, end, 0 if b == 0 else rows - 1, 1, c * chunk, chunk, ebo.at[c, b])

    def pots(c, b):
        return out(S, pot, 0 if b == 0 else rows - 1, 1, c * chunk, chunk, pbo.at[c, b])

    end_inner = out(E, end, 1, inner, 0, width, eo)
    pot_inner = out(S, pot, 1, inner, 0, width, po)

    @pl.loop(0, chunks)
    def _(c):
        for d in (0, 1):
            start(ay.sends[d], ycopy(0, d, c))
    for d in (0, 1):
        start(ax.sends[d], xcopy(0, d))
    loads[0].wait()
    for d in (0, 1):
        start(az.sends[d], zcopy(0, d))

        @pl.loop(0, chunks)
        def _(c):
            for b in (0, 1):
                start(az.sends[d], zbcopy(0, d, c, b))
    for copy in loads[1:]:
        copy.wait()

    subs = width // sub
    for t in range(STEPS):
        for d in (0, 1):
            arrived(ax.gets[d], xcopy(t, d))
            arrived(az.gets[d], zcopy(t, d))

        @pl.loop(0, inner * subs)
        def _(i):
            cells(t, 1 + i // subs, (i % subs) * sub)

        if t < STEPS - 1:
            for d in (0, 1):
                start(az.sends[d], zcopy(t + 1, d))
        else:
            end_inner.start()

            @pl.when(az.gets[1])
            def _():
                zcopy(STEPS, 1).wait_recv()

                @pl.loop(0, inner * subs)
                def _(i):
                    add_below(1 + i // subs, (i % subs) * sub)
            start(az.sends[1], zcopy(STEPS, 1))
            pot_inner.start()

        @pl.loop(0, chunks)
        def _(c):
            for d in (0, 1):
                arrived(ay.gets[d], ycopy(t, d, c))
                for b in (0, 1):
                    arrived(az.gets[d], zbcopy(t, d, c, b))
            for b, y in ((0, 0), (1, rows - 1)):
                @pl.loop(0, chunk // sub)
                def _(i):
                    cells(t, y, c * chunk + i * sub)
                if t < STEPS - 1:
                    start(ay.sends[b], ycopy(t + 1, b, c))
                    for d in (0, 1):
                        start(az.sends[d], zbcopy(t + 1, d, c, b))
                else:
                    ends(c, b).start()

        if t < STEPS - 1:
            for d in (0, 1):
                start(ax.sends[d], xcopy(t + 1, d))

    @pl.loop(0, chunks)
    def _(c):
        for b, y in ((0, 0), (1, rows - 1)):
            @pl.when(az.gets[1])
            def _():
                zbcopy(STEPS, 1, c, b).wait_recv()

                @pl.loop(0, chunk // sub)
                def _(i):
                    add_below(y, c * chunk + i * sub)
            start(az.sends[1], zbcopy(STEPS, 1, c, b))
            pots(c, b).start()

    def left(flag, copy):
        @pl.when(flag)
        def _():
            copy.wait_send()

    for t in range(STEPS + 1):
        for d in (0, 1):
            if t < STEPS:
                left(ax.sends[d], xcopy(t, d))
            if t < STEPS or d == 1:
                left(az.sends[d], zcopy(t, d))

        @pl.loop(0, chunks)
        def _(c):
            for d in (0, 1):
                if t < STEPS:
                    left(ay.sends[d], ycopy(t, d, c))
                if t < STEPS or d == 1:
                    for b in (0, 1):
                        left(az.sends[d], zbcopy(t, d, c, b))
    end_inner.wait()
    pot_inner.wait()

    @pl.loop(0, chunks)
    def _(c):
        for b in (0, 1):
            ends(c, b).wait()
            pots(c, b).wait()


def local(counts, tracer, flow_y, flow_x, flow_z):
    rows, width, depth, lanes = tracer.shape
    chunk = divisor(width, 16)
    sub = divisor(chunk, 8)
    chunks = width // chunk
    block = jax.ShapeDtypeStruct(tracer.shape, jnp.float32)
    dma = pltpu.SemaphoreType.DMA
    return pl.pallas_call(
        functools.partial(kernel, counts, chunk, sub),
        out_shape=(block, block),
        in_specs=[pl.BlockSpec(memory_space=pl.ANY)] * 4,
        out_specs=[pl.BlockSpec(memory_space=pl.ANY)] * 2,
        scratch_shapes=[
            pltpu.VMEM((STEPS, rows + 2, width + 2, depth, lanes), jnp.float32),
            pltpu.VMEM(tracer.shape, jnp.float32),
            pltpu.VMEM(tracer.shape, jnp.float32),
            pltpu.VMEM((3,) + tracer.shape, jnp.float32),
            pltpu.VMEM((STEPS + 1,) + tracer.shape, jnp.float32),
            dma((4,)),
            dma((STEPS, 2, chunks)),
            dma((STEPS, 2, chunks)),
            dma((STEPS, 2)),
            dma((STEPS, 2)),
            dma((STEPS + 1, 2)),
            dma((STEPS + 1, 2)),
            dma((STEPS + 1, 2, chunks, 2)),
            dma((STEPS + 1, 2, chunks, 2)),
            dma(()),
            dma(()),
            dma((chunks, 2)),
            dma((chunks, 2)),
        ],
        compiler_params=pltpu.CompilerParams(
            collective_id=0, has_side_effects=True, vmem_limit_bytes=60 * 1024 * 1024
        ),
    )(tracer, flow_y, flow_x, flow_z)


def solution(mesh):
    counts = tuple(mesh.shape[name] for name in ("py", "px", "pz"))
    placed = P("py", "px", "pz", None)
    return jax.shard_map(
        functools.partial(local, counts),
        mesh=mesh,
        in_specs=(placed,) * 4,
        out_specs=(placed, placed),
        check_vma=False,
    )
```

time: 196 us -> 83.8 us (0.43); the launches traced: 193 us -> 83.4 us
  Pallas kernels: 0 us -> 77.2 us
  waiting for transfers between devices: 69.9 us -> 0 us
  starting transfers between devices: 68.2 us -> 0 us
  other arithmetic: 39.5 us -> 0 us
  local copies, waits for them, and re-layouts: 11.7 us -> 5.6 us
  blocking collectives: 2.5 us -> 0 us
    pallas_call x0 -> x1, Pallas kernels: none -> 77.2 us  [local(): pl.pallas_call(functools.partial(kernel, counts, chunk, sub), out_shape=(...]
    ppermute x24 -> x0, waiting for transfers between devices: 69.9 us -> none  [the longest x12 42.7 us: padded_2(): lax.ppermute(lax.slice_in_dim(block, block.shape[dim] - width, None, axis...]
    ppermute x24 -> x0, starting transfers between devices: 68.2 us -> none  [the longest x12 35 us: padded_2(): lax.ppermute(lax.slice_in_dim(block, block.shape[dim] - width, None, axis...]
    add x5 -> x0, other arithmetic: 34.3 us -> none  [the longest x4 33.9 us: one_step(): middle - flow_y * slopes[0] - flow_x * slopes[1] - flow_z * slopes[2]]
    unnamed x21 -> x4, local copies, waits for them, and re-layouts: 10.1 us -> 5.6 us
    another operation x1 -> x0, other arithmetic: 3.29 us -> none  [local(): here = jnp.cumsum(tracer, axis=2)]
    all_gather x1 -> x0, blocking collectives: 2.5 us -> none  [prefix(): gathered = lax.all_gather(part, axis)]
  transfers between devices with their start and end apart: 24 -> 0, of which waited for: 19 -> 0; matrix products, arithmetic and copies ran while one was open for 0% -> 0% of each run, Pallas kernels for 0% -> 0%
where the time goes in v1:
time: 83.8 us; the launch traced here: 83.4 us
  Pallas kernels  77.2 us (92%)
  local copies, waits for them, and re-layouts  5.6 us (7%)
    pallas_call x1, Pallas kernels, local(): pl.pallas_call(functools.partial(kernel, counts, chunk, sub), out_shape=(...  77.2 us
    unnamed x4, local copies, waits for them, and re-layouts  5.6 us

profile of v1, /device:TPU:5, one launch (start us, length us, event | category | flops | bytes accessed | tf_op | source)
XLA Modules:
  0.0 83.4 jit_solution(18380960691759934096)
XLA Ops:
  0.6 77.2 %shard_map.59 = (f32[8,96,8,128]{3,2,1,0:T(8,128)}, f32[8,96,8,128]{3,2,1,0:T(8,128)}) custom-call(f32[8,96,8,128]{3,2,1,0:T(8,128)} %tr.1, f32[8,96,8,128]{3,2,1,0:T(8,128)} %fy.1, f32[8,96,8,128]{3,2,1,0:T(8,128)} %fx.1, f32[8,96,8,128]{3,2,1,0:T(8,128)} %fz.1), custom_call_target="tpu_custom_call" | custom-call | tf_op jit(solution)/shard_map/pallas_call | solution.py:274
  77.8 0.0 copy-start
  77.8 3.9 %copy.8 = f32[8,96,8,128]{3,2,1,0:T(8,128)} copy(f32[8,96,8,128]{3,2,1,0:T(8,128)} %get-tuple-element.4) | data formatting | bytes 6291456
  81.8 0.0 copy-done
  81.8 1.7 %copy.9 = f32[8,96,8,128]{3,2,1,0:T(8,128)} copy(f32[8,96,8,128]{3,2,1,0:T(8,128)S(1)} %copy-done) | data formatting | bytes 6291456
Async XLA Ops:
  77.8 3.9 %copy-start = (f32[8,96,8,128]{3,2,1,0:T(8,128)S(1)}, f32[8,96,8,128]{3,2,1,0:T(8,128)}, u32[]{:S(2)}) copy-start(f32[8,96,8,128]{3,2,1,0:T(8,128)} %get-tuple-element.5) | copy-start | bytes 9437188

commit v2 on v1

--- a/solution.py
+++ b/solution.py
@@ -24,12 +24,13 @@
         self.gets = (self.sends[1], self.sends[0])
 
 
-def kernel(counts, chunk, sub, tr, fy, fx, fz, pot, end, T, E, S, F, Z, load, ys, yr, xs, xr, zs, zr, zbs, zbr, eo, po, ebo, pbo):
+def kernel(counts, relays, chunk, sub, tr, fy, fx, fz, S, E, T, F, Z, R, load, rs, rr, ys, yr, xs, xr, zs, zr, zbs, zbr):
     rows, width, depth, lanes = tr.shape
     chunks = width // chunk
     ay, ax, az = (Axis(n, c) for n, c in zip(("py", "px", "pz"), counts))
     flows = (fy, fx, fz)
     inner = rows - 2
+    direct = chunks // 2
 
     loads = [pltpu.make_async_copy(tr, T.at[0, pl.ds(1, rows), pl.ds(1, width)], load.at[0])]
     loads += [pltpu.make_async_copy(f, F.at[i], load.at[1 + i]) for i, f in enumerate(flows)]
@@ -44,6 +45,15 @@
             def _():
                 pl.semaphore_signal(barrier, inc=1, device_id={axis.name: axis.to[d]}, device_id_type=MESH)
             expect = expect + axis.sends[d].astype(jnp.int32)
+    pairs = {frozenset((a, r)) for a, d, r in relays} | {frozenset((r, a + 2 * d - 1)) for a, d, r in relays}
+    for one, other in sorted(sorted(p) for p in pairs):
+        if other - one == 1:
+            continue
+        for a, b in ((one, other), (other, one)):
+            @pl.when(ay.me == a)
+            def _():
+                pl.semaphore_signal(barrier, inc=1, device_id={"py": b}, device_id_type=MESH)
+            expect = expect + (ay.me == a).astype(jnp.int32)
 
     def blank(t):
         for d in (0, 1):
@@ -61,20 +71,45 @@
         blank(t)
     pl.semaphore_wait(barrier, expect)
 
-    def remote(src, dst, ssem, rsem, axis, d):
+    def remote(src, dst, ssem, rsem, axis, d, to=None):
         return pltpu.make_async_remote_copy(
             src_ref=src, dst_ref=dst, send_sem=ssem, recv_sem=rsem,
-            device_id={axis.name: axis.to[d]}, device_id_type=MESH,
+            device_id={axis.name: axis.to[d] if to is None else to}, device_id_type=MESH,
         )
 
-    def ycopy(t, d, c):
+    def ycopy(t, d, c, relay=None):
         at = c * chunk
         if t == 0:
             src = tr.at[0 if d == 0 else rows - 1, pl.ds(at, chunk)]
         else:
             src = T.at[t, 1 if d == 0 else rows, pl.ds(1 + at, chunk)]
+        if relay is not None:
+            return remote(src, R.at[t, pl.ds(at, chunk)], ys.at[t, d, c], rr.at[t, c], ay, d, relay)
         dst = T.at[t, rows + 1 if d == 0 else 0, pl.ds(1 + at, chunk)]
         return remote(src, dst, ys.at[t, d, c], yr.at[t, d, c], ay, d)
+
+    def ysend(t, d, c):
+        plain = ay.sends[d]
+        for a, way, relay in relays:
+            if way == d:
+                turn = (ay.me == a) & (c >= direct)
+                plain = plain & jnp.logical_not(turn)
+                start(turn, ycopy(t, d, c, relay))
+        start(plain, ycopy(t, d, c))
+
+    def passed(t, a, d, c):
+        at = c * chunk
+        dst = T.at[t, rows + 1 if d == 0 else 0, pl.ds(1 + at, chunk)]
+        return remote(R.at[t, pl.ds(at, chunk)], dst, rs.at[t, c], yr.at[t, d, c], ay, d, a + 2 * d - 1)
+
+    def pass_on(t):
+        for a, d, relay in relays:
+            @pl.when(ay.me == relay)
+            def _():
+                @pl.loop(direct, chunks)
+                def _(c):
+                    ycopy(t, d, c, relay).wait_recv()
+                    passed(t, a, d, c).start()
 
     def xcopy(t, d):
         if t == 0:
@@ -143,24 +178,10 @@
         low = Z[STEPS, y, pl.ds(x, sub), pl.ds(depth - 1, 1)]
         S[y, pl.ds(x, sub)] = S[y, pl.ds(x, sub)] + low
 
-    def out(ref, to, y, ny, x, nx, sem):
-        return pltpu.make_async_copy(
-            ref.at[pl.ds(y, ny), pl.ds(x, nx)], to.at[pl.ds(y, ny), pl.ds(x, nx)], sem
-        )
-
-    def ends(c, b):
-        return out(E, end, 0 if b == 0 else rows - 1, 1, c * chunk, chunk, ebo.at[c, b])
-
-    def pots(c, b):
-        return out(S, pot, 0 if b == 0 else rows - 1, 1, c * chunk, chunk, pbo.at[c, b])
-
-    end_inner = out(E, end, 1, inner, 0, width, eo)
-    pot_inner = out(S, pot, 1, inner, 0, width, po)
-
     @pl.loop(0, chunks)
     def _(c):
         for d in (0, 1):
-            start(ay.sends[d], ycopy(0, d, c))
+            ysend(0, d, c)
     for d in (0, 1):
         start(ax.sends[d], xcopy(0, d))
     loads[0].wait()
@@ -171,6 +192,7 @@
         def _(c):
             for b in (0, 1):
                 start(az.sends[d], zbcopy(0, d, c, b))
+    pass_on(0)
     for copy in loads[1:]:
         copy.wait()
 
@@ -188,8 +210,6 @@
             for d in (0, 1):
                 start(az.sends[d], zcopy(t + 1, d))
         else:
-            end_inner.start()
-
             @pl.when(az.gets[1])
             def _():
                 zcopy(STEPS, 1).wait_recv()
@@ -198,7 +218,8 @@
                 def _(i):
                     add_below(1 + i // subs, (i % subs) * sub)
             start(az.sends[1], zcopy(STEPS, 1))
-            pot_inner.start()
+        if t > 0:
+            pass_on(t)
 
         @pl.loop(0, chunks)
         def _(c):
@@ -211,11 +232,9 @@
                 def _(i):
                     cells(t, y, c * chunk + i * sub)
                 if t < STEPS - 1:
-                    start(ay.sends[b], ycopy(t + 1, b, c))
+                    ysend(t + 1, b, c)
                     for d in (0, 1):
                         start(az.sends[d], zbcopy(t + 1, d, c, b))
-                else:
-                    ends(c, b).start()
 
         if t < STEPS - 1:
             for d in (0, 1):
@@ -232,12 +251,19 @@
                 def _(i):
                     add_below(y, c * chunk + i * sub)
             start(az.sends[1], zbcopy(STEPS, 1, c, b))
-            pots(c, b).start()
 
     def left(flag, copy):
         @pl.when(flag)
         def _():
             copy.wait_send()
+
+    for a, d, relay in relays:
+        @pl.when(ay.me == relay)
+        def _():
+            for t in range(STEPS):
+                @pl.loop(direct, chunks)
+                def _(c):
+                    passed(t, a, d, c).wait_send()
 
     for t in range(STEPS + 1):
         for d in (0, 1):
@@ -254,35 +280,28 @@
                 if t < STEPS or d == 1:
                     for b in (0, 1):
                         left(az.sends[d], zbcopy(t, d, c, b))
-    end_inner.wait()
-    pot_inner.wait()
-
-    @pl.loop(0, chunks)
-    def _(c):
-        for b in (0, 1):
-            ends(c, b).wait()
-            pots(c, b).wait()
-
-
-def local(counts, tracer, flow_y, flow_x, flow_z):
+
+
+def local(counts, relays, tracer, flow_y, flow_x, flow_z):
     rows, width, depth, lanes = tracer.shape
     chunk = divisor(width, 16)
     sub = divisor(chunk, 8)
     chunks = width // chunk
-    block = jax.ShapeDtypeStruct(tracer.shape, jnp.float32)
+    block = pltpu.VMEM(tracer.shape, jnp.float32)
     dma = pltpu.SemaphoreType.DMA
     return pl.pallas_call(
-        functools.partial(kernel, counts, chunk, sub),
+        functools.partial(kernel, counts, relays, chunk, sub),
         out_shape=(block, block),
         in_specs=[pl.BlockSpec(memory_space=pl.ANY)] * 4,
-        out_specs=[pl.BlockSpec(memory_space=pl.ANY)] * 2,
+        out_specs=[pl.BlockSpec(memory_space=pltpu.VMEM)] * 2,
         scratch_shapes=[
             pltpu.VMEM((STEPS, rows + 2, width + 2, depth, lanes), jnp.float32),
-            pltpu.VMEM(tracer.shape, jnp.float32),
-            pltpu.VMEM(tracer.shape, jnp.float32),
             pltpu.VMEM((3,) + tracer.shape, jnp.float32),
             pltpu.VMEM((STEPS + 1,) + tracer.shape, jnp.float32),
+            pltpu.VMEM((STEPS, width, depth, lanes), jnp.float32),
             dma((4,)),
+            dma((STEPS, chunks)),
+            dma((STEPS, chunks)),
             dma((STEPS, 2, chunks)),
             dma((STEPS, 2, chunks)),
             dma((STEPS, 2)),
@@ -291,22 +310,40 @@
             dma((STEPS + 1, 2)),
             dma((STEPS + 1, 2, chunks, 2)),
             dma((STEPS + 1, 2, chunks, 2)),
-            dma(()),
-            dma(()),
-            dma((chunks, 2)),
-            dma((chunks, 2)),
         ],
         compiler_params=pltpu.CompilerParams(
-            collective_id=0, has_side_effects=True, vmem_limit_bytes=60 * 1024 * 1024
+            collective_id=0, has_side_effects=True, vmem_limit_bytes=50 * 1024 * 1024
         ),
     )(tracer, flow_y, flow_x, flow_z)
+
+
+KEEP = 0
+
+
+def detours(mesh):
+    spots = [getattr(device, "coords", None) for device in mesh.devices[:, 0, 0]]
+    if any(spot is None for spot in spots):
+        return ()
+    gap = lambda a, b: [i for i, (p, q) in enumerate(zip(spots[a], spots[b])) if p != q]
+    found, busy = [], set()
+    for a in range(len(spots)):
+        for d, b in ((0, a - 1), (1, a + 1)):
+            if not 0 <= b < len(spots) or len(gap(a, b)) != 2:
+                continue
+            kept, other = gap(a, b)[KEEP], gap(a, b)[1 - KEEP]
+            for r in range(len(spots)):
+                if r not in busy and gap(a, r) == [other] and gap(r, b) == [kept]:
+                    busy.add(r)
+                    found.append((a, d, r))
+                    break
+    return tuple(found)
 
 
 def solution(mesh):
     counts = tuple(mesh.shape[name] for name in ("py", "px", "pz"))
     placed = P("py", "px", "pz", None)
     return jax.shard_map(
-        functools.partial(local, counts),
+        functools.partial(local, counts, detours(mesh)),
         mesh=mesh,
         in_specs=(placed,) * 4,
         out_specs=(placed, placed),

time: 83.8 us -> 65.4 us (0.78)
  Pallas kernels: 77.2 us -> 61.3 us
  local copies, waits for them, and re-layouts: 5.6 us -> 3.33 us
    pallas_call x1, Pallas kernels: 77.2 us -> 61.3 us  [local(): pl.pallas_call(functools.partial(kernel, counts, relays, chunk, sub), out...]
    unnamed x4 -> x2, local copies, waits for them, and re-layouts: 5.6 us -> 3.33 us
where the time goes in v2:
time: 65.4 us; the launch traced here: 65.3 us
  Pallas kernels  61.3 us (94%)
  local copies, waits for them, and re-layouts  3.33 us (5%)
    pallas_call x1, Pallas kernels, local(): pl.pallas_call(functools.partial(kernel, counts, relays, chunk, sub), out...  61.3 us
    unnamed x2, local copies, waits for them, and re-layouts  3.33 us

profile of v2, /device:TPU:5, one launch (start us, length us, event | category | flops | bytes accessed | tf_op | source)
XLA Modules:
  0.0 65.3 jit_solution(14102818633214600565)
XLA Ops:
  0.6 61.3 %shard_map.59 = (f32[8,96,8,128]{3,2,1,0:T(8,128)S(1)}, f32[8,96,8,128]{3,2,1,0:T(8,128)S(1)}) custom-call(f32[8,96,8,128]{3,2,1,0:T(8,128)} %tr.1, f32[8,96,8,128]{3,2,1,0:T(8,128)} %fy.1, f32[8,96,8,128]{3,2,1,0:T(8,128)} %fx.1, f32[8,96,8,128]{3,2,1,0:T(8,128)} %fz.1), custom_call_target="tpu_custom_call" | custom-call | tf_op jit(solution)/shard_map/pallas_call | solution.py:292
  62.0 1.7 %copy.8 = f32[8,96,8,128]{3,2,1,0:T(8,128)} copy(f32[8,96,8,128]{3,2,1,0:T(8,128)S(1)} %get-tuple-element.2) | data formatting | bytes 6291456
  63.6 1.7 %copy.9 = f32[8,96,8,128]{3,2,1,0:T(8,128)} copy(f32[8,96,8,128]{3,2,1,0:T(8,128)S(1)} %get-tuple-element.3) | data formatting | bytes 6291456

commit v3 on v2

--- a/solution.py
+++ b/solution.py
@@ -32,9 +32,12 @@
     inner = rows - 2
     direct = chunks // 2
 
-    loads = [pltpu.make_async_copy(tr, T.at[0, pl.ds(1, rows), pl.ds(1, width)], load.at[0])]
-    loads += [pltpu.make_async_copy(f, F.at[i], load.at[1 + i]) for i, f in enumerate(flows)]
-    for copy in loads:
+    loads = [
+        pltpu.make_async_copy(tr.at[pl.ds(y, n)], T.at[0, pl.ds(1 + y, n), pl.ds(1, width)], load.at[i])
+        for i, (y, n) in enumerate(((0, 1), (rows - 1, 1), (1, inner)))
+    ]
+    loads += [pltpu.make_async_copy(f, F.at[i], load.at[3 + i]) for i, f in enumerate(flows)]
+    for copy in loads[:3]:
         copy.start()
 
     barrier = pltpu.get_barrier_semaphore()
@@ -79,20 +82,20 @@
 
     def ycopy(t, d, c, relay=None):
         at = c * chunk
-        if t == 0:
-            src = tr.at[0 if d == 0 else rows - 1, pl.ds(at, chunk)]
-        else:
-            src = T.at[t, 1 if d == 0 else rows, pl.ds(1 + at, chunk)]
+        src = T.at[t, 1 if d == 0 else rows, pl.ds(1 + at, chunk)]
         if relay is not None:
             return remote(src, R.at[t, pl.ds(at, chunk)], ys.at[t, d, c], rr.at[t, c], ay, d, relay)
         dst = T.at[t, rows + 1 if d == 0 else 0, pl.ds(1 + at, chunk)]
         return remote(src, dst, ys.at[t, d, c], yr.at[t, d, c], ay, d)
 
+    def detoured(t):
+        return (direct, chunks) if t == 0 else (0, direct)
+
     def ysend(t, d, c):
         plain = ay.sends[d]
         for a, way, relay in relays:
             if way == d:
-                turn = (ay.me == a) & (c >= direct)
+                turn = (ay.me == a) & ((c >= direct) if t == 0 else (c < direct))
                 plain = plain & jnp.logical_not(turn)
                 start(turn, ycopy(t, d, c, relay))
         start(plain, ycopy(t, d, c))
@@ -106,16 +109,13 @@
         for a, d, relay in relays:
             @pl.when(ay.me == relay)
             def _():
-                @pl.loop(direct, chunks)
+                @pl.loop(*detoured(t))
                 def _(c):
                     ycopy(t, d, c, relay).wait_recv()
                     passed(t, a, d, c).start()
 
     def xcopy(t, d):
-        if t == 0:
-            src = tr.at[:, pl.ds(0 if d == 0 else width - 1, 1)]
-        else:
-            src = T.at[t, pl.ds(1, rows), pl.ds(1 if d == 0 else width, 1)]
+        src = T.at[t, pl.ds(1, rows), pl.ds(1 if d == 0 else width, 1)]
         dst = T.at[t, pl.ds(1, rows), pl.ds(width + 1 if d == 0 else 0, 1)]
         return remote(src, dst, xs.at[t, d], xr.at[t, d], ax, d)
 
@@ -178,13 +178,27 @@
         low = Z[STEPS, y, pl.ds(x, sub), pl.ds(depth - 1, 1)]
         S[y, pl.ds(x, sub)] = S[y, pl.ds(x, sub)] + low
 
+    def finish(c):
+        for b, y in ((0, 0), (1, rows - 1)):
+            zbcopy(STEPS, 1, c, b).wait_recv()
+
+            @pl.loop(0, chunk // sub)
+            def _(i):
+                add_below(y, c * chunk + i * sub)
+            start(az.sends[1], zbcopy(STEPS, 1, c, b))
+
+    loads[0].wait()
+    loads[1].wait()
+
     @pl.loop(0, chunks)
     def _(c):
         for d in (0, 1):
             ysend(0, d, c)
+    for copy in loads[3:]:
+        copy.start()
+    loads[2].wait()
     for d in (0, 1):
         start(ax.sends[d], xcopy(0, d))
-    loads[0].wait()
     for d in (0, 1):
         start(az.sends[d], zcopy(0, d))
 
@@ -193,7 +207,7 @@
             for b in (0, 1):
                 start(az.sends[d], zbcopy(0, d, c, b))
     pass_on(0)
-    for copy in loads[1:]:
+    for copy in loads[3:]:
         copy.wait()
 
     subs = width // sub
@@ -218,11 +232,12 @@
                 def _(i):
                     add_below(1 + i // subs, (i % subs) * sub)
             start(az.sends[1], zcopy(STEPS, 1))
-        if t > 0:
-            pass_on(t)
-
         @pl.loop(0, chunks)
         def _(c):
+            if t < STEPS - 1:
+                @pl.when(c == direct)
+                def _():
+                    pass_on(t + 1)
             for d in (0, 1):
                 arrived(ay.gets[d], ycopy(t, d, c))
                 for b in (0, 1):
@@ -235,22 +250,20 @@
                     ysend(t + 1, b, c)
                     for d in (0, 1):
                         start(az.sends[d], zbcopy(t + 1, d, c, b))
+                else:
+                    start(az.sends[1] & jnp.logical_not(az.gets[1]), zbcopy(STEPS, 1, c, b))
+            if t == STEPS - 1:
+                @pl.when(az.gets[1] & (c > 0))
+                def _():
+                    finish(c - 1)
 
         if t < STEPS - 1:
             for d in (0, 1):
                 start(ax.sends[d], xcopy(t + 1, d))
 
-    @pl.loop(0, chunks)
-    def _(c):
-        for b, y in ((0, 0), (1, rows - 1)):
-            @pl.when(az.gets[1])
-            def _():
-                zbcopy(STEPS, 1, c, b).wait_recv()
-
-                @pl.loop(0, chunk // sub)
-                def _(i):
-                    add_below(y, c * chunk + i * sub)
-            start(az.sends[1], zbcopy(STEPS, 1, c, b))
+    @pl.when(az.gets[1])
+    def _():
+        finish(chunks - 1)
 
     def left(flag, copy):
         @pl.when(flag)
@@ -261,7 +274,7 @@
         @pl.when(ay.me == relay)
         def _():
             for t in range(STEPS):
-                @pl.loop(direct, chunks)
+                @pl.loop(*detoured(t))
                 def _(c):
                     passed(t, a, d, c).wait_send()
 
@@ -284,7 +297,7 @@
 
 def local(counts, relays, tracer, flow_y, flow_x, flow_z):
     rows, width, depth, lanes = tracer.shape
-    chunk = divisor(width, 16)
+    chunk = divisor(width, 48)
     sub = divisor(chunk, 8)
     chunks = width // chunk
     block = pltpu.VMEM(tracer.shape, jnp.float32)
@@ -299,7 +312,7 @@
             pltpu.VMEM((3,) + tracer.shape, jnp.float32),
             pltpu.VMEM((STEPS + 1,) + tracer.shape, jnp.float32),
             pltpu.VMEM((STEPS, width, depth, lanes), jnp.float32),
-            dma((4,)),
+            dma((6,)),
             dma((STEPS, chunks)),
             dma((STEPS, chunks)),
             dma((STEPS, 2, chunks)),

time: 65.4 us -> 62.4 us (0.954)
  Pallas kernels: 61.3 us -> 57.7 us
    pallas_call x1, Pallas kernels: 61.3 us -> 57.7 us  [local(): pl.pallas_call(functools.partial(kernel, counts, relays, chunk, sub), out...]
where the time goes in v3:
time: 62.4 us; the launch traced here: 61.7 us
  Pallas kernels  57.7 us (92%)
  local copies, waits for them, and re-layouts  3.33 us (5%)
  between operations  0.64 us (1%)
    pallas_call x1, Pallas kernels, local(): pl.pallas_call(functools.partial(kernel, counts, relays, chunk, sub), out...  57.7 us
    unnamed x2, local copies, waits for them, and re-layouts  3.33 us

profile of v3, /device:TPU:5, one launch (start us, length us, event | category | flops | bytes accessed | tf_op | source)
XLA Modules:
  0.0 61.7 jit_solution(2677310844946335906)
XLA Ops:
  0.6 57.7 %shard_map.59 = (f32[8,96,8,128]{3,2,1,0:T(8,128)S(1)}, f32[8,96,8,128]{3,2,1,0:T(8,128)S(1)}) custom-call(f32[8,96,8,128]{3,2,1,0:T(8,128)} %tr.1, f32[8,96,8,128]{3,2,1,0:T(8,128)} %fy.1, f32[8,96,8,128]{3,2,1,0:T(8,128)} %fx.1, f32[8,96,8,128]{3,2,1,0:T(8,128)} %fz.1), custom_call_target="tpu_custom_call" | custom-call | tf_op jit(solution)/shard_map/pallas_call | solution.py:305
  58.3 1.7 %copy.8 = f32[8,96,8,128]{3,2,1,0:T(8,128)} copy(f32[8,96,8,128]{3,2,1,0:T(8,128)S(1)} %get-tuple-element.2) | data formatting | bytes 6291456
  60.0 1.7 %copy.9 = f32[8,96,8,128]{3,2,1,0:T(8,128)} copy(f32[8,96,8,128]{3,2,1,0:T(8,128)S(1)} %get-tuple-element.3) | data formatting | bytes 6291456

commit v4 on v3

--- a/solution.py
+++ b/solution.py
@@ -37,7 +37,7 @@
         for i, (y, n) in enumerate(((0, 1), (rows - 1, 1), (1, inner)))
     ]
     loads += [pltpu.make_async_copy(f, F.at[i], load.at[3 + i]) for i, f in enumerate(flows)]
-    for copy in loads[:3]:
+    for copy in loads:
         copy.start()
 
     barrier = pltpu.get_barrier_semaphore()
@@ -194,8 +194,6 @@
     def _(c):
         for d in (0, 1):
             ysend(0, d, c)
-    for copy in loads[3:]:
-        copy.start()
     loads[2].wait()
     for d in (0, 1):
         start(ax.sends[d], xcopy(0, d))
@@ -298,7 +296,7 @@
 def local(counts, relays, tracer, flow_y, flow_x, flow_z):
     rows, width, depth, lanes = tracer.shape
     chunk = divisor(width, 48)
-    sub = divisor(chunk, 8)
+    sub = divisor(chunk, 12)
     chunks = width // chunk
     block = pltpu.VMEM(tracer.shape, jnp.float32)
     dma = pltpu.SemaphoreType.DMA

time: 62.4 us -> 61.8 us (level)
  no operation moved by 1% of the time
where the time goes in v4:
time: 61.8 us; the launch traced here: 61.6 us
  Pallas kernels  57.7 us (93%)
  local copies, waits for them, and re-layouts  3.33 us (5%)
  between operations  0.64 us (1%)
    pallas_call x1, Pallas kernels, local(): pl.pallas_call(functools.partial(kernel, counts, relays, chunk, sub), out...  57.7 us
    unnamed x2, local copies, waits for them, and re-layouts  3.33 us

profile of v4, /device:TPU:5, one launch (start us, length us, event | category | flops | bytes accessed | tf_op | source)
XLA Modules:
  0.0 61.6 jit_solution(7716792591149411193)
XLA Ops:
  0.6 57.7 %shard_map.59 = (f32[8,96,8,128]{3,2,1,0:T(8,128)S(1)}, f32[8,96,8,128]{3,2,1,0:T(8,128)S(1)}) custom-call(f32[8,96,8,128]{3,2,1,0:T(8,128)} %tr.1, f32[8,96,8,128]{3,2,1,0:T(8,128)} %fy.1, f32[8,96,8,128]{3,2,1,0:T(8,128)} %fx.1, f32[8,96,8,128]{3,2,1,0:T(8,128)} %fz.1), custom_call_target="tpu_custom_call" | custom-call | tf_op jit(solution)/shard_map/pallas_call | solution.py:303
  58.3 1.7 %copy.8 = f32[8,96,8,128]{3,2,1,0:T(8,128)} copy(f32[8,96,8,128]{3,2,1,0:T(8,128)S(1)} %get-tuple-element.2) | data formatting | bytes 6291456
  60.0 1.7 %copy.9 = f32[8,96,8,128]{3,2,1,0:T(8,128)} copy(f32[8,96,8,128]{3,2,1,0:T(8,128)S(1)} %get-tuple-element.3) | data formatting | bytes 6291456
